TPU v7x, 256 devices: a 4x2x16 block of a 4x16x16 slice. The times are simulated.
256 devices in a mesh: groups: 2 (over y), dp: 32 (over z, core), expert: 4 (over x).
Axes of the slice: x: 4, y: 2, z: 16, core: 2. Of those that a mesh axis runs over, the one named last changes fastest.
The devices are a block of a 4x16x16 slice.
Arguments:
- queries: bfloat16 [2, 1024, 32, 128], P(None, ('groups', 'dp'), 'expert'), parts along dimension 1, may hold values from -6 to 6
- fresh_kv: bfloat16 [2, 1024, 4, 256], P(None, ('groups', 'dp'), 'expert'), parts along dimension 1, may hold values from -6 to 6
- kv_pool: bfloat16 [20480, 16, 4, 256], P(('groups', 'dp'), None, 'expert'), parts along dimension 0, may hold values from -6 to 6
- page_table: int32 [1024, 305], P(('groups', 'dp')), parts along dimension 0, may hold values from -1 to 319, as said below
- context_lengths: int32 [1024], P(('groups', 'dp')), parts along dimension 0, may hold values from 1 to 4880, as said below
- residual: bfloat16 [2, 1024, 4096], P(None, ('groups', 'dp'), 'expert'), parts along dimension 1, may hold values from -16 to 16
- out_weight: bfloat16 [4096, 4096], P('expert', 'dp'), may hold values from -0.09375 to 0.09375
- norm_gain: float32 [4096], P('expert'), may hold values from 0.1 to 1.9
- expert_ids: int32 [2, 1024, 8], P(None, ('groups', 'dp')), parts along dimension 1, may hold values from 0 to 63, all different within a row; in each aligned block of 16 rows (0 to 15, 16 to 31, ..., all dimensions but the last counted through in order) at most 5 rows name the same one
- route_weights: float32 [2, 1024, 8], P(None, ('groups', 'dp')), parts along dimension 1, may hold values from 0.1 to 1
- gate_up: bfloat16 [64, 2, 4096, 768], P('dp', None, 'expert'), may hold values from -0.09375 to 0.09375
- down_proj: bfloat16 [64, 768, 4096], P('dp', None, 'expert'), may hold values from -0.21875 to 0.21875
Outputs:
- layer_out: bfloat16 [2, 1024, 4096], P(None, ('groups', 'dp'), 'expert'), parts along dimension 1
There are 2 independent parts, one for each index of `groups`. A program takes and returns all parts, laid end to end along the dimension named above; an argument that names none is the same for every part. Nothing has to cross between parts.
Inputs may be any that keep to these rules, and one draw needn't show every extreme that they name: `page_table`: entries 0 to ceil(context_lengths[i] / 16) - 1 of a row name distinct pages, no page is named twice within the 16 requests of one block, and later entries are -1. The requests of one block hold at most 320 pages together; in every draw some block holds exactly 320, and some request holds exactly 305 pages. `context_lengths`: every request holds at least one cached token; in every draw some request holds exactly 4880. `expert_ids`: within the rows of one device (16 requests of one step) no expert is named by more than 5 rows.
All inputs are finite; a program needn't handle non-finite values.
Results may differ from a plain program's by a relative error of at most 0.005.
Values may be sent and summed in bfloat16 or wider, within the bound.
A program may use at most 64 MiB of HBM per device.

v0:
```python
import math
import jax
import jax.numpy as jnp
from jax import lax
from jax.sharding import PartitionSpec as P

NEG = -1e30
EPS = 1e-06
EXACT = lax.Precision.HIGHEST


def in_blocks(array, dim, length):
    before, after = (array.shape[:dim], array.shape[dim + 1 :])
    return jnp.moveaxis(array.reshape(*before, length, -1, *after), dim, 0)


def summed_on_arrival(array, axis, dim):
    length = lax.axis_size(axis)
    pieces = lax.all_to_all(in_blocks(array, dim, length), axis, 0, 0, tiled=True)
    return jnp.sum(pieces.astype(jnp.float32), axis=0)


def in_one_piece(arrays, axis, dim, along):
    both = jnp.concatenate(arrays, axis=along)
    whole, at, outs = (summed_on_arrival(both, axis, dim), 0, [])
    for a in arrays:
        outs.append(lax.slice_in_dim(whole, at, at + a.shape[along], axis=along))
        at += a.shape[along]
    return tuple(outs)


def page_owners(table, lengths, pool_pages, page_len):
    pages = jnp.arange(pool_pages, dtype=jnp.int32)
    matches = table[:, :, None] == pages[None, None, :]
    ownership = jnp.any(matches, axis=1)
    slot_index = jnp.arange(table.shape[1], dtype=jnp.int32)
    position = jnp.sum(jnp.where(matches, slot_index[None, :, None], 0), axis=(0, 1))
    owner_length = jnp.sum(jnp.where(ownership, lengths[:, None], 0), axis=0)
    live_count = jnp.clip(owner_length - position * page_len, 0, page_len)
    return (ownership, live_count)


def attend(query_block, fresh_block, pool_block, table_block, length_block):
    step_count, req_count, head_count, head_width = query_block.shape
    pool_pages, page_len, kv_heads, _ = pool_block.shape
    group_size = head_count // kv_heads
    score_scale = 1.0 / math.sqrt(head_width)
    ownership, live_count = page_owners(table_block, length_block, pool_pages, page_len)
    owned_f = ownership.astype(jnp.float32)
    grouped = query_block.reshape(step_count, req_count, kv_heads, group_size, head_width)
    page_query = jnp.einsum(
        "rp,srkgd->pskgd",
        ownership.astype(jnp.bfloat16),
        grouped,
        preferred_element_type=jnp.float32,
    ).astype(jnp.bfloat16)
    key_rows = pool_block[..., :head_width]
    value_rows = pool_block[..., head_width:]
    page_scores = (
        jnp.einsum("pskgd,ptkd->pskgt", page_query, key_rows, preferred_element_type=jnp.float32)
        * score_scale
    )
    in_page = jnp.arange(page_len)[None, :] < live_count[:, None]
    page_scores = jnp.where(in_page[:, None, None, None, :], page_scores, NEG)
    fresh_keys = fresh_block[..., :head_width]
    fresh_values = fresh_block[..., head_width:]
    fresh_scores = (
        jnp.einsum("srkgd,urkd->srkgu", grouped, fresh_keys, preferred_element_type=jnp.float32)
        * score_scale
    )
    causal = jnp.arange(step_count)[:, None] >= jnp.arange(step_count)[None, :]
    fresh_scores = jnp.where(causal[:, None, None, None, :], fresh_scores, NEG)
    page_best = jnp.max(page_scores, axis=4)
    row_best = jnp.max(jnp.where(ownership[:, :, None, None, None], page_best[None], NEG), axis=1)
    row_best = jnp.maximum(row_best, jnp.moveaxis(jnp.max(fresh_scores, axis=4), 0, 1))
    owner_best = jnp.einsum("rp,rskg->pskg", owned_f, row_best, precision=EXACT)
    page_probs = jnp.exp(page_scores - owner_best[..., None])
    page_sum = jnp.sum(page_probs, axis=4)
    page_acc = jnp.einsum(
        "pskgt,ptkd->pskgd",
        page_probs.astype(jnp.bfloat16),
        value_rows,
        preferred_element_type=jnp.float32,
    )
    denominator = jnp.einsum("rp,pskg->rskg", owned_f, page_sum, precision=EXACT)
    numerator = jnp.einsum("rp,pskgd->rskgd", owned_f, page_acc, precision=EXACT)
    fresh_probs = jnp.exp(fresh_scores - jnp.moveaxis(row_best, 1, 0)[..., None])
    denominator = denominator + jnp.moveaxis(jnp.sum(fresh_probs, axis=4), 0, 1)
    numerator = numerator + jnp.einsum(
        "srkgu,urkd->rskgd",
        fresh_probs.astype(jnp.bfloat16),
        fresh_values,
        preferred_element_type=jnp.float32,
    )
    attended = jnp.moveaxis(numerator / denominator[..., None], 1, 0)
    return attended.reshape(step_count, req_count, head_count * head_width).astype(jnp.bfloat16)


def dispatch_keys(expert_ids, expert_total, local_experts, dp_count, capacity):
    step_count = expert_ids.shape[0]
    catalog = jnp.arange(expert_total, dtype=jnp.int32)
    named_mask = jnp.any(expert_ids[..., None] == catalog, axis=2).astype(jnp.int32)
    earlier = jnp.cumsum(named_mask, axis=1) - named_mask
    slot_rank = jnp.take_along_axis(earlier, expert_ids, axis=2)
    owner_index = expert_ids // local_experts
    local_index = expert_ids % local_experts
    step_index = jnp.arange(step_count, dtype=jnp.int32)[:, None, None]
    return ((local_index * dp_count + owner_index) * step_count + step_index) * capacity + slot_rank


def body(
    queries,
    fresh_kv,
    kv_pool,
    page_table,
    context_lengths,
    residual,
    out_weight,
    norm_gain,
    expert_ids,
    route_weights,
    gate_up,
    down_proj,
):
    attended = attend(queries, fresh_kv, kv_pool, page_table, context_lengths)
    step_count, req_count, head_cols = attended.shape
    flat_attended = attended.reshape(step_count * req_count, head_cols)
    partial_out = jnp.dot(
        flat_attended,
        lax.all_gather(out_weight, "dp", axis=1, tiled=True),
        preferred_element_type=jnp.float32,
    )
    projected = summed_on_arrival(partial_out.astype(jnp.bfloat16), "expert", 1)
    quarter = projected.shape[1]
    stream = residual.astype(jnp.float32).reshape(step_count * req_count, quarter) + projected
    squares = lax.psum(jnp.sum(stream * stream, axis=1), "expert")
    model_width = quarter * lax.axis_size("expert")
    inverse = lax.rsqrt(squares / model_width + EPS)
    normed = (stream * inverse[:, None] * norm_gain[None, :]).astype(jnp.bfloat16)
    dp_count = lax.axis_size("dp")
    local_experts = gate_up.shape[0]
    expert_total = local_experts * dp_count
    top_count = expert_ids.shape[2]
    capacity = min(
        req_count, max(2, (5 * req_count * top_count + 2 * expert_total - 1) // (2 * expert_total))
    )
    slot_keys = dispatch_keys(expert_ids, expert_total, local_experts, dp_count, capacity)
    slot_total = local_experts * dp_count * step_count * capacity
    slot_ids = jnp.arange(slot_total, dtype=jnp.int32)
    chosen = slot_keys.reshape(step_count * req_count, top_count)[None] == slot_ids[:, None, None]
    selector = jnp.any(chosen, axis=2).astype(jnp.bfloat16)
    outgoing = jnp.dot(selector, normed, preferred_element_type=jnp.float32).astype(jnp.bfloat16)
    outgoing = outgoing.reshape(local_experts, dp_count, step_count * capacity, quarter)
    incoming = lax.all_to_all(outgoing, "dp", split_axis=1, concat_axis=1, tiled=True)
    expert_rows = incoming.reshape(local_experts, dp_count * step_count * capacity, quarter)
    gate_part = jnp.einsum(
        "jmd,jdh->jmh", expert_rows, gate_up[:, 0], preferred_element_type=jnp.float32
    )
    up_part = jnp.einsum(
        "jmd,jdh->jmh", expert_rows, gate_up[:, 1], preferred_element_type=jnp.float32
    )
    gate_share, up_share = in_one_piece(
        (gate_part.astype(jnp.bfloat16), up_part.astype(jnp.bfloat16)), "expert", 2, 0
    )
    active_share = (jax.nn.silu(gate_share) * up_share).astype(jnp.bfloat16)
    activated = lax.all_gather(active_share, "expert", axis=2, tiled=True)
    expert_out = jnp.einsum(
        "jmh,jhd->jmd", activated, down_proj, preferred_element_type=jnp.float32
    ).astype(jnp.bfloat16)
    expert_out = expert_out.reshape(local_experts, dp_count, step_count * capacity, quarter)
    returned = lax.all_to_all(expert_out, "dp", split_axis=1, concat_axis=1, tiled=True)
    returned = returned.reshape(slot_total, quarter)
    picked = returned[slot_keys].astype(jnp.float32)
    share = route_weights / jnp.sum(route_weights, axis=2, keepdims=True)
    mixture = jnp.sum(share[..., None] * picked, axis=2)
    return (stream.reshape(step_count, req_count, quarter) + mixture).astype(jnp.bfloat16)


def solution(mesh):
    return jax.shard_map(
        body,
        mesh=mesh,
        in_specs=(
            P(None, ("groups", "dp"), "expert", None),
            P(None, ("groups", "dp"), "expert", None),
            P(("groups", "dp"), None, "expert", None),
            P(("groups", "dp"), None),
            P(("groups", "dp")),
            P(None, ("groups", "dp"), "expert"),
            P("expert", "dp"),
            P("expert"),
            P(None, ("groups", "dp"), None),
            P(None, ("groups", "dp"), None),
            P("dp", None, "expert", None),
            P("dp", None, "expert"),
        ),
        out_specs=P(None, ("groups", "dp"), "expert"),
        check_vma=False,
    )
```

profile of v0, /device:TPU:33, one launch (start us, length us, event | category | flops | bytes accessed | tf_op | source)
XLA Modules:
  0.0 385.2 jit_solution(539590098517076246)
XLA Ops:
  6.6 0.7 all-gather.2.cloned.1.call-update
  7.3 1.0 copy.119
  8.3 1.2 fusion
  9.5 0.7 select_reduce_fusion.2
  10.3 1.5 select_reduce_fusion
  11.9 1.4 convolution_convert_fusion.1
  13.3 4.5 %fusion.12 = (f32[320,2,8]{2,1,0:T(2,128)S(1)}, f32[320,2,8,16]{3,2,1,0:T(8,128)}) fusion(pred[320,16]{1,0:T(8,128)(4,1)S(1)} %iota_compare_fusion.2, bf16[320,16,1,256]{3,1,0,2:T(8,128)(2,1)} %bitcast.199, bf16[320,2,8,128]{3,0,2,1:T(8,128)(2,1)S(1)} %convolution_convert_fusion.1), kind=kOutput, calls=%fused_computation.20 | convolution fusion | flops 21212160 | bytes 2974720 | tf_op jit(solution)/shard_map/pskgd,ptkd->pskgt/dot_general | solution.py:60
  17.8 0.8 copy.123
  18.5 0.9 select_reduce_fusion.1
  20.0 1.9 fusion.86
  22.6 0.7 convolution_bitcast_fusion
  23.3 0.9 copy.127
  24.2 3.9 %fusion.10 = f32[320,2,8]{2,1,0:T(2,128)} fusion(f32[320,2,8,16]{3,2,1,0:T(8,128)} %get-tuple-element.12, f32[320,2,8]{2,1,0:T(2,128)S(1)} %copy.127, pred[320,16]{1,0:T(8,128)(4,1)S(1)} %iota_compare_fusion.2), kind=kLoop, calls=%fused_computation.18 | loop fusion | flops 322560 | bytes 373760 | tf_op jit(solution)/shard_map/reduce_sum | solution.py:78
  28.1 1.7 copy.132
  29.8 0.7 fusion.74
  30.6 0.8 fusion.63
  32.1 0.9 fusion.47
  32.9 1.0 fusion.66
  33.9 3.0 fusion.20
  37.0 1.6 fusion.42
  39.0 2.4 gather_fusion.1
  41.6 76.4 %all-gather.2.cloned.1.call-done = bf16[1024,4096]{1,0:T(8,128)(2,1)} async-done(((bf16[1024,128]{1,0:T(8,128)(2,1)}), bf16[1024,4096]{1,0:T(8,128)(2,1)}) %all-gather.2.cloned.1.call-update) | async-done | bytes 8388624 | tf_op jit(solution)/shard_map/all_gather | solution.py:130
  118.0 4.9 %convolution_convert_fusion = bf16[32,4096]{1,0:T(8,128)(2,1)S(1)} fusion(bf16[1024,4096]{1,0:T(8,128)(2,1)} %all-gather.2.cloned.1.call-done, bf16[4,8,8,128]{3,2,1,0:T(8,128)(2,1)S(1)} %bitcast.201), kind=kOutput, calls=%fused_computation.6 | convolution fusion | flops 268566528 | bytes 8716288 | tf_op jit(solution)/shard_map/dot_general | solution.py:128
  123.6 4.0 %all-to-all-start = ((bf16[4,32,1024]{2,1,0:T(8,128)(2,1)}), bf16[4,32,1024]{2,1,0:T(8,128)(2,1)S(1)}, u32[]{:S(2)}, u32[]{:S(2)}) async-start(bf16[4,32,1024]{2,1,0:T(8,128)(2,1)} %bitcast.198), calls=%async_computation | async-start | bytes 524288 | tf_op jit(solution)/shard_map/all_to_all | solution.py:19
  127.7 0.9 fusion.50
  128.6 5.0 %all-to-all-done = bf16[4,32,1024]{2,1,0:T(8,128)(2,1)S(1)} async-done(((bf16[4,32,1024]{2,1,0:T(8,128)(2,1)}), bf16[4,32,1024]{2,1,0:T(8,128)(2,1)S(1)}, u32[]{:S(2)}, u32[]{:S(2)}) %all-to-all-start) | async-done | bytes 262176 | tf_op jit(solution)/shard_map/all_to_all | solution.py:19
  133.6 0.9 multiply_reduce_fusion
  134.6 7.1 %psum.7 = f32[32]{0:T(128)S(1)} all-reduce(f32[32]{0:T(128)S(1)} %reduce_sum.96), channel_id=1, replica_groups=mesh['groups'=2,'dp'=32,'expert'=4] {'expert'}, use_global_device_ids=true, to_apply=%region_14.15 | all-reduce | flops 32 | bytes 256 | tf_op jit(solution)/shard_map/psum | solution.py:136
  141.7 0.9 fusion.54
  142.6 2.3 convolution_convert_fusion.3
  145.0 3.6 reshape.165
  148.6 3.1 copy.146
  151.7 78.1 %all_to_all.20 = bf16[2,32,10,1024]{3,0,2,1:T(2,128)(2,1)S(1)} all-to-all(bf16[2,32,10,1024]{3,0,2,1:T(2,128)(2,1)S(1)} %copy.146), channel_id=1, replica_groups=mesh['groups'=2,'dp'=32,'expert'=4] {'dp'}, dimensions={1} | all-to-all | bytes 2621440 | tf_op jit(solution)/shard_map/all_to_all | solution.py:154
  229.8 3.2 fusion.13
  233.0 1.2 fusion.16
  234.2 1.4 pad_maximum_fusion
  235.7 4.1 %copy.151 = bf16[4,320,768]{1,2,0:T(8,128)(2,1)} copy(bf16[4,320,768]{2,1,0:T(8,128)(2,1)} %pad_maximum_fusion) | data formatting | bytes 3932160 | tf_op jit(solution)/shard_map/concatenate | solution.py:24
  239.8 1.9 copy.152
  241.7 31.3 %all_to_all.21 = bf16[4,4,320,192]{2,3,1,0:T(8,128)(2,1)S(1)} all-to-all(bf16[4,4,320,192]{2,3,1,0:T(8,128)(2,1)S(1)} %copy.152), channel_id=1, replica_groups=mesh['groups'=2,'dp'=32,'expert'=4] {'expert'}, dimensions={0} | all-to-all | bytes 3932160 | tf_op jit(solution)/shard_map/all_to_all | solution.py:19
  273.6 12.4 %all_gather.7 = bf16[2,320,768]{1,2,0:T(8,128)(2,1)S(1)} all-gather(bf16[2,320,192]{1,2,0:T(8,128)(2,1)S(1)} %fusion.51), channel_id=1, replica_groups=mesh['groups'=2,'dp'=32,'expert'=4] {'expert'}, dimensions={2}, use_global_device_ids=true | all-gather | bytes 1228800 | tf_op jit(solution)/shard_map/all_gather | solution.py:166
  286.0 1.2 convolution_convert_fusion.2
  287.3 2.4 copy.153
  289.7 9.1 %all-to-all-start.3 = ((bf16[2,32,10,1024]{3,0,2,1:T(2,128)(2,1)}), bf16[2,32,10,1024]{3,0,2,1:T(2,128)(2,1)}, u32[]{:S(2)}, u32[]{:S(2)}) async-start(bf16[2,32,10,1024]{3,0,2,1:T(2,128)(2,1)} %bitcast.193), calls=%async_computation.3 | async-start | bytes 2621440 | tf_op jit(solution)/shard_map/all_to_all | solution.py:171
  299.0 66.6 %all-to-all-done.3 = bf16[2,32,10,1024]{3,0,2,1:T(2,128)(2,1)} async-done(((bf16[2,32,10,1024]{3,0,2,1:T(2,128)(2,1)}), bf16[2,32,10,1024]{3,0,2,1:T(2,128)(2,1)}, u32[]{:S(2)}, u32[]{:S(2)}) %all-to-all-start.3) | async-done | bytes 1310752 | tf_op jit(solution)/shard_map/all_to_all | solution.py:171
  365.6 3.2 copy.154
  368.8 3.6 reshape.169
  372.4 3.9 %gather_fusion = bf16[256,1024]{1,0:T(8,128)(2,1)} fusion(bf16[640,1024]{1,0:T(8,128)(2,1)} %reshape.169, s32[1024]{0:T(1024)S(1)} %pad_clamp_fusion), kind=kCustom, calls=%fused_computation | custom fusion | bytes 1049600 | tf_op jit(solution)/shard_map/gather | solution.py:173
  376.3 1.4 fusion.49
  (47 shorter events, 4.9 us)
Async XLA Ops:
  6.5 279.4 %copy-start = (bf16[2,768,1024]{2,1,0:T(8,128)(2,1)S(1)}, bf16[2,768,1024]{2,1,0:T(8,128)(2,1)}, u32[]{:S(2)}) copy-start(bf16[2,768,1024]{2,1,0:T(8,128)(2,1)} %param.23) | copy-start | bytes 9437188
  6.6 111.4 %all-gather.2.cloned.1.call-start = ((), (), s32[]{:S(2)}) async-start(), calls=%async_computation.4 | async-start | bytes 8650752 | tf_op jit(solution)/shard_map/all_gather | solution.py:130
  13.3 6.1 %copy-start.4 = (bf16[2,16,1,256]{3,1,2,0:T(8,128)(2,1)S(1)}, bf16[2,16,1,256]{3,1,2,0:T(8,128)(2,1)}, u32[]{:S(2)}) copy-start(bf16[2,16,1,256]{3,1,2,0:T(8,128)(2,1)} %param.13) | copy-start | bytes 49156
  21.9 0.6 copy-start.2
  37.0 1.7 copy-start.5
  123.6 9.9 %all-to-all-start = ((bf16[4,32,1024]{2,1,0:T(8,128)(2,1)}), bf16[4,32,1024]{2,1,0:T(8,128)(2,1)S(1)}, u32[]{:S(2)}, u32[]{:S(2)}) async-start(bf16[4,32,1024]{2,1,0:T(8,128)(2,1)} %bitcast.198), calls=%async_computation | async-start | bytes 524288 | tf_op jit(solution)/shard_map/all_to_all | solution.py:19
  148.6 84.4 %slice-start = ((s8[6291456]{0:T(1024)(128)(4,1)}), s8[2097152]{0:T(1024)(128)(4,1)S(1)}, s32[]{:S(2)}) async-start(s8[6291456]{0:T(1024)(128)(4,1)} %bitcast.203), calls=%async_computation.5 | async-start | bytes 4194304
  229.8 3.2 slice-start.1
  287.2 11.6 %copy-start.3 = (f32[2,16,8]{1,2,0:T(8,128)S(1)}, f32[2,16,8]{1,2,0:T(8,128)}, u32[]{:S(2)}) copy-start(f32[2,16,8]{1,2,0:T(8,128)} %param.21) | copy-start | bytes 3076
  289.7 75.9 %all-to-all-start.3 = ((bf16[2,32,10,1024]{3,0,2,1:T(2,128)(2,1)}), bf16[2,32,10,1024]{3,0,2,1:T(2,128)(2,1)}, u32[]{:S(2)}, u32[]{:S(2)}) async-start(bf16[2,32,10,1024]{3,0,2,1:T(2,128)(2,1)} %bitcast.193), calls=%async_computation.3 | async-start | bytes 2621440 | tf_op jit(solution)/shard_map/all_to_all | solution.py:171
  372.4 5.3 %copy-start.1 = (bf16[2,16,1024]{2,1,0:T(8,128)(2,1)S(1)}, bf16[2,16,1024]{2,1,0:T(8,128)(2,1)}, u32[]{:S(2)}) copy-start(bf16[2,16,1024]{2,1,0:T(8,128)(2,1)} %param.17) | copy-start | bytes 196612
Sparse Core Ops, SparseCore 0:
  9.1 108.8 all-gather.1
where the time goes:
time: 387 us; the launch traced here: 385 us
  waiting for transfers between devices  149 us (39%)
  blocking collectives  129 us (33%)
  local copies, waits for them, and re-layouts  35.8 us (9%)
  matrix products  27.9 us (7%)
  other arithmetic  17 us (4%)
  between operations  13.7 us (4%)
  starting transfers between devices  13.1 us (3%)
    all_to_all x1, blocking collectives, body(): lax.all_to_all(outgoing, 'dp', split_axis=1, concat_axis=1, tiled=True)  78.1 us
    all_gather x1, waiting for transfers between devices, body(): lax.all_gather(out_weight, 'dp', axis=1, tiled=True)  76.4 us
    all_to_all x1, waiting for transfers between devices, body(): lax.all_to_all(expert_out, 'dp', split_axis=1, concat_axis=1, tiled=True)  66.6 us
    all_to_all x1, blocking collectives, summed_on_arrival(): lax.all_to_all(in_blocks(array, dim, length), axis, 0, 0, tiled=True)  31.3 us
    all_gather x1, blocking collectives, body(): activated = lax.all_gather(active_share, 'expert', axis=2, tiled=True)  12.4 us
    all_to_all x1, starting transfers between devices, body(): lax.all_to_all(expert_out, 'dp', split_axis=1, concat_axis=1, tiled=True)  9.08 us
  transfers between devices with their start and end apart: 3, of which 3 were waited for; matrix products, arithmetic and copies ran while one was open for 9% of the time, Pallas kernels for 0%

commit v1 on v0

--- a/solution.py
+++ b/solution.py
@@ -127,7 +127,9 @@
     flat_attended = attended.reshape(step_count * req_count, head_cols)
     partial_out = jnp.dot(
         flat_attended,
-        lax.all_gather(out_weight, "dp", axis=1, tiled=True),
+        jnp.concatenate(
+            lax.all_to_all(jnp.stack([out_weight] * lax.axis_size("dp")), "dp", 0, 0), axis=1
+        ),
         preferred_element_type=jnp.float32,
     )
     projected = summed_on_arrival(partial_out.astype(jnp.bfloat16), "expert", 1)

time: 387 us -> 660 us (1.71)
  waiting for transfers between devices: 149 us -> 397 us
  starting transfers between devices: 13.1 us -> 39.2 us
  between operations: 13.7 us -> 0.35 us
  local copies, waits for them, and re-layouts: 35.8 us -> 42.4 us
    all_to_all x0 -> x1, waiting for transfers between devices: none -> 327 us  [body(): lax.all_to_all(jnp.stack([out_weight] * lax.axis_size('dp')), 'dp', 0, 0)]
    all_gather x1 -> x0, waiting for transfers between devices: 76.4 us -> none  [body(): lax.all_gather(out_weight, 'dp', axis=1, tiled=True)]
    all_to_all x0 -> x1, starting transfers between devices: none -> 25.6 us  [body(): lax.all_to_all(jnp.stack([out_weight] * lax.axis_size('dp')), 'dp', 0, 0)]
  transfers between devices with their start and end apart: 3 -> 3, of which waited for: 3 -> 3; matrix products, arithmetic and copies ran while one was open for 9% -> 5% of each run, Pallas kernels for 0% -> 0%
where the time goes in v1:
time: 660 us; the launch traced here: 658 us
  waiting for transfers between devices  397 us (60%)
  blocking collectives  134 us (20%)
  local copies, waits for them, and re-layouts  42.4 us (6%)
  starting transfers between devices  39.2 us (6%)
  matrix products  28.1 us (4%)
  other arithmetic  16.9 us (3%)
    all_to_all x1, waiting for transfers between devices, body(): lax.all_to_all(jnp.stack([out_weight] * lax.axis_size('dp')), 'dp', 0, 0)  327 us
    all_to_all x1, blocking collectives, body(): lax.all_to_all(outgoing, 'dp', split_axis=1, concat_axis=1, tiled=True)  83.5 us
    all_to_all x1, waiting for transfers between devices, body(): lax.all_to_all(expert_out, 'dp', split_axis=1, concat_axis=1, tiled=True)  66.6 us
    all_to_all x1, blocking collectives, summed_on_arrival(): lax.all_to_all(in_blocks(array, dim, length), axis, 0, 0, tiled=True)  31.3 us
    all_to_all x1, starting transfers between devices, body(): lax.all_to_all(jnp.stack([out_weight] * lax.axis_size('dp')), 'dp', 0, 0)  25.6 us
  transfers between devices with their start and end apart: 3, of which 3 were waited for; matrix products, arithmetic and copies ran while one was open for 5% of the time, Pallas kernels for 0%

profile of v1, /device:TPU:33, one launch (start us, length us, event | category | flops | bytes accessed | tf_op | source)
XLA Modules:
  0.0 658.3 jit_solution(16739225165646645850)
XLA Ops:
  0.0 1.2 copy.138
  1.2 4.3 stack.2
  5.5 25.6 %all-to-all-start = ((bf16[32,1024,128]{1,2,0:T(8,128)(2,1)}), bf16[32,1024,128]{1,2,0:T(8,128)(2,1)}, u32[]{:S(2)}, u32[]{:S(2)}) async-start(bf16[32,1024,128]{1,2,0:T(8,128)(2,1)} %stack.2), calls=%async_computation | async-start | bytes 16777216 | tf_op jit(solution)/shard_map/all_to_all | solution.py:131
  31.6 2.4 gather_fusion.1
  34.8 1.2 fusion
  36.1 1.5 select_reduce_fusion
  38.3 4.4 fusion.12
  42.7 0.8 copy.126
  43.4 0.9 select_reduce_fusion.1
  44.3 1.3 fusion.85
  45.6 1.9 fusion.86
  48.2 0.7 convolution_bitcast_fusion
  48.9 0.9 copy.130
  49.8 3.9 fusion.10
  53.7 1.7 copy.135
  56.8 0.8 fusion.63
  58.3 0.9 fusion.47
  59.1 1.0 fusion.66
  60.1 3.0 fusion.20
  63.2 1.7 fusion.42
  64.9 326.6 %all-to-all-done = bf16[32,1024,128]{1,2,0:T(8,128)(2,1)} async-done(((bf16[32,1024,128]{1,2,0:T(8,128)(2,1)}), bf16[32,1024,128]{1,2,0:T(8,128)(2,1)}, u32[]{:S(2)}, u32[]{:S(2)}) %all-to-all-start) | async-done | bytes 8388640 | tf_op jit(solution)/shard_map/all_to_all | solution.py:131
  391.4 5.9 convolution_convert_fusion
  397.3 0.7 copy.209
  398.1 4.5 all-to-all-start.1
  403.2 0.9 fusion.50
  404.1 4.2 all-to-all-done.1
  408.3 0.9 multiply_reduce_fusion
  409.4 6.9 %psum.7 = f32[32]{0:T(128)S(1)} all-reduce(f32[32]{0:T(128)S(1)} %reduce_sum.96), channel_id=1, replica_groups=mesh['groups'=2,'dp'=32,'expert'=4] {'expert'}, use_global_device_ids=true, to_apply=%region_14.15 | all-reduce | flops 32 | bytes 256 | tf_op jit(solution)/shard_map/psum | solution.py:138
  416.2 0.9 fusion.54
  417.2 2.3 convolution_convert_fusion.3
  419.5 3.6 reshape.175
  423.1 3.1 copy.150
  426.2 83.5 %all_to_all.25 = bf16[2,32,10,1024]{3,0,2,1:T(2,128)(2,1)S(1)} all-to-all(bf16[2,32,10,1024]{3,0,2,1:T(2,128)(2,1)S(1)} %copy.150), channel_id=1, replica_groups=mesh['groups'=2,'dp'=32,'expert'=4] {'dp'}, dimensions={1} | all-to-all | bytes 2621440 | tf_op jit(solution)/shard_map/all_to_all | solution.py:156
  509.7 3.2 fusion.16
  512.9 1.2 fusion.13
  514.1 1.4 pad_maximum_fusion
  515.6 4.1 copy.155
  519.7 1.9 copy.156
  521.6 31.3 %all_to_all.26 = bf16[4,4,320,192]{2,3,1,0:T(8,128)(2,1)S(1)} all-to-all(bf16[4,4,320,192]{2,3,1,0:T(8,128)(2,1)S(1)} %copy.156), channel_id=1, replica_groups=mesh['groups'=2,'dp'=32,'expert'=4] {'expert'}, dimensions={0} | all-to-all | bytes 3932160 | tf_op jit(solution)/shard_map/all_to_all | solution.py:19
  553.5 12.4 %all_gather.3 = bf16[2,320,768]{1,2,0:T(8,128)(2,1)S(1)} all-gather(bf16[2,320,192]{1,2,0:T(8,128)(2,1)S(1)} %fusion.51), channel_id=1, replica_groups=mesh['groups'=2,'dp'=32,'expert'=4] {'expert'}, dimensions={2}, use_global_device_ids=true | all-gather | bytes 1228800 | tf_op jit(solution)/shard_map/all_gather | solution.py:168
  565.9 1.2 convolution_convert_fusion.2
  567.2 2.4 copy.157
  569.6 9.1 %all-to-all-start.4 = ((bf16[2,32,10,1024]{3,0,2,1:T(2,128)(2,1)}), bf16[2,32,10,1024]{3,0,2,1:T(2,128)(2,1)}, u32[]{:S(2)}, u32[]{:S(2)}) async-start(bf16[2,32,10,1024]{3,0,2,1:T(2,128)(2,1)} %bitcast.196), calls=%async_computation.4 | async-start | bytes 2621440 | tf_op jit(solution)/shard_map/all_to_all | solution.py:173
  578.9 66.6 %all-to-all-done.4 = bf16[2,32,10,1024]{3,0,2,1:T(2,128)(2,1)} async-done(((bf16[2,32,10,1024]{3,0,2,1:T(2,128)(2,1)}), bf16[2,32,10,1024]{3,0,2,1:T(2,128)(2,1)}, u32[]{:S(2)}, u32[]{:S(2)}) %all-to-all-start.4) | async-done | bytes 1310752 | tf_op jit(solution)/shard_map/all_to_all | solution.py:173
  645.5 3.2 copy.158
  648.7 3.6 reshape.179
  652.3 3.9 gather_fusion
  656.2 1.4 fusion.49
  (58 shorter events, 6.8 us)
Async XLA Ops:
  0.0 565.9 %copy-start = (bf16[2,768,1024]{2,1,0:T(8,128)(2,1)S(1)}, bf16[2,768,1024]{2,1,0:T(8,128)(2,1)}, u32[]{:S(2)}) copy-start(bf16[2,768,1024]{2,1,0:T(8,128)(2,1)} %param.23) | copy-start | bytes 9437188
  5.5 25.6 %copy-start.9 = (s32[2,16,8]{1,2,0:T(8,128)S(1)}, s32[2,16,8]{1,2,0:T(8,128)}, u32[]{:S(2)}) copy-start(s32[2,16,8]{1,2,0:T(8,128)} %param.20) | copy-start | bytes 3076
  5.5 385.9 %all-to-all-start = ((bf16[32,1024,128]{1,2,0:T(8,128)(2,1)}), bf16[32,1024,128]{1,2,0:T(8,128)(2,1)}, u32[]{:S(2)}, u32[]{:S(2)}) async-start(bf16[32,1024,128]{1,2,0:T(8,128)(2,1)} %stack.2), calls=%async_computation | async-start | bytes 16777216 | tf_op jit(solution)/shard_map/all_to_all | solution.py:131
  31.5 3.2 copy-start.8
  31.5 4.5 copy-start.10
  31.5 6.2 copy-start.6
  47.5 0.6 copy-start.3
  56.2 0.6 copy-start.2
  391.4 11.2 %copy-start.4 = (s32[2,16,8]{2,1,0:T(8,128)S(1)}, s32[2,16,8]{2,1,0:T(8,128)}, u32[]{:S(2)}) copy-start(s32[2,16,8]{2,1,0:T(8,128)} %reshape.191) | copy-start | bytes 3076
  398.1 10.2 %all-to-all-start.1 = ((bf16[4,32,1024]{2,1,0:T(8,128)(2,1)}), bf16[4,32,1024]{2,1,0:T(8,128)(2,1)S(1)}, u32[]{:S(2)}, u32[]{:S(2)}) async-start(bf16[4,32,1024]{2,1,0:T(8,128)(2,1)} %bitcast.201), calls=%async_computation.1 | async-start | bytes 524288 | tf_op jit(solution)/shard_map/all_to_all | solution.py:19
  423.1 89.8 %slice-start = ((s8[6291456]{0:T(1024)(128)(4,1)}), s8[2097152]{0:T(1024)(128)(4,1)S(1)}, s32[]{:S(2)}) async-start(s8[6291456]{0:T(1024)(128)(4,1)} %bitcast.206), calls=%async_computation.5 | async-start | bytes 4194304
  509.7 3.2 slice-start.1
  567.2 11.5 %copy-start.7 = (f32[2,16,8]{1,2,0:T(8,128)S(1)}, f32[2,16,8]{1,2,0:T(8,128)}, u32[]{:S(2)}) copy-start(f32[2,16,8]{1,2,0:T(8,128)} %param.21) | copy-start | bytes 3076
  567.2 11.6 %copy-start.5 = (s32[2,16,8]{2,1,0:T(8,128)S(1)}, s32[2,16,8]{2,1,0:T(8,128)}, u32[]{:S(2)}) copy-start(s32[2,16,8]{2,1,0:T(8,128)} %get-tuple-element.5) | copy-start | bytes 3076
  569.6 75.9 %all-to-all-start.4 = ((bf16[2,32,10,1024]{3,0,2,1:T(2,128)(2,1)}), bf16[2,32,10,1024]{3,0,2,1:T(2,128)(2,1)}, u32[]{:S(2)}, u32[]{:S(2)}) async-start(bf16[2,32,10,1024]{3,0,2,1:T(2,128)(2,1)} %bitcast.196), calls=%async_computation.4 | async-start | bytes 2621440 | tf_op jit(solution)/shard_map/all_to_all | solution.py:173
  652.3 5.3 copy-start.1
